TPU v7x, 32 devices: a whole 2x2x4 slice. The times are simulated.
32 devices in a mesh: grp: 4 (over x, core), feat: 8 (over z, y).
Axes of the slice: x: 2, y: 2, z: 4, core: 2. Of those that a mesh axis runs over, the one named last changes fastest.
Arguments:
- resid: bfloat16 [4, 128, 4096], P('grp', 'feat'), may hold values from -600 to 600
- norm_gain: float32 [4, 4096], P('grp'), may hold values from 0.25 to 1.75
- w_gate: bfloat16 [4, 4096, 14336], P('grp', None, 'feat'), may hold values from -0.09375 to 0.09375
- w_up: bfloat16 [4, 4096, 14336], P('grp', None, 'feat'), may hold values from -0.09375 to 0.09375
- w_down: bfloat16 [4, 14336, 4096], P('grp', 'feat'), may hold values from -0.046875 to 0.046875
- w_enc: bfloat16 [4, 4096, 16384], P('grp', None, 'feat'), may hold values from -0.09375 to 0.09375
- b_enc: float32 [4, 16384], P('grp', 'feat'), may hold values from -0.8 to 0.2
- w_dec: bfloat16 [4, 16384, 8192], P('grp', 'feat'), may hold values from -0.046875 to 0.046875
- carry_in: float32 [128, 4096], P('feat'), may hold values from -3 to 3
Outputs:
- errors: float32 [4, 128, 4096], P('grp', 'feat')
- forward: float32 [4, 128, 4096], P('grp', 'feat')
All inputs are finite; a program needn't handle non-finite values.
Results may differ from a plain program's by a relative error of at most 0.0044.
Values may be sent and summed in bfloat16 or wider, within the bound.
A program may use at most 192 MiB of HBM per device.

v0:
```python
import jax
import jax.numpy as jnp
from jax import lax
from jax.sharding import PartitionSpec as P


def passed_along(value, axis, steps):
    count = lax.axis_size(axis)
    initial, last = (max(0, -steps), min(count, count - steps))
    return lax.ppermute(value, axis, [(source, source + steps) for source in range(initial, last)])


def body(resid, norm_gain, w_gate, w_up, w_down, w_enc, b_enc, w_dec, carry_in):
    stream = resid[0].astype(jnp.float32)
    inv_rms = lax.rsqrt(jnp.mean(stream * stream, axis=1, keepdims=True) + 1e-05)
    normed = (stream * inv_rms * norm_gain[0]).astype(jnp.bfloat16)
    gate_cols = w_gate[0]
    up_cols = w_up[0]
    enc_cols = w_enc[0]
    enc_bias = b_enc[0]
    hidden_width = gate_cols.shape[1]
    tile_rows = lax.all_gather(normed, "feat", axis=0, tiled=True)
    gate_sum = jnp.dot(tile_rows, gate_cols, preferred_element_type=jnp.float32)
    up_sum = jnp.dot(tile_rows, up_cols, preferred_element_type=jnp.float32)
    hidden_part = (jax.nn.silu(gate_sum) * up_sum).astype(jnp.bfloat16)
    pre_act = jnp.dot(tile_rows, enc_cols, preferred_element_type=jnp.float32) + enc_bias
    feature_part = jax.nn.relu(pre_act).astype(jnp.bfloat16)
    joined = jnp.concatenate([hidden_part, feature_part], axis=1)
    hidden = joined[:, :hidden_width]
    features = joined[:, hidden_width:]
    down_rows = w_down[0]
    dec_rows = w_dec[0]
    model_width = down_rows.shape[1]
    dec_part = jnp.dot(features, dec_rows, preferred_element_type=jnp.float32)
    mlp_part = jnp.dot(hidden, down_rows, preferred_element_type=jnp.float32)
    decoded = lax.psum_scatter(
        jnp.concatenate([dec_part[:, :model_width] - mlp_part, dec_part[:, model_width:]], axis=1),
        "feat",
        scatter_dimension=0,
        tiled=True,
    )
    own_error = decoded[:, :model_width]
    to_next = decoded[:, model_width:]
    passed = passed_along(to_next, "grp", 1)
    incoming = jnp.where(lax.axis_index("grp") == 0, carry_in, passed)
    err_rows = own_error + incoming
    return (err_rows[None], to_next[None])


def solution(mesh):
    return jax.shard_map(
        body,
        mesh=mesh,
        in_specs=(
            P("grp", "feat", None),
            P("grp", None),
            P("grp", None, "feat"),
            P("grp", None, "feat"),
            P("grp", "feat", None),
            P("grp", None, "feat"),
            P("grp", "feat"),
            P("grp", "feat", None),
            P("feat", None),
        ),
        out_specs=(P("grp", "feat", None), P("grp", "feat", None)),
        check_vma=False,
    )
```

profile of v0, /device:TPU:0, one launch (start us, length us, event | category | flops | bytes accessed | tf_op | source)
XLA Modules:
  0.0 205.2 jit_solution(5915634257625057729)
XLA Ops:
  7.2 0.0 all-gather.2.cloned.1.call-start
  7.2 1.1 fusion.31
  8.3 1.7 fusion.33
  9.9 0.0 all-gather.2.cloned.1.call-update
  10.0 0.0 reduce-scatter.2.cloned.1.call-start
  10.0 43.7 %all-gather.2.cloned.1.call-done = bf16[128,4096]{1,0:T(8,128)(2,1)} async-done(((bf16[16,4096]{1,0:T(8,128)(2,1)}), bf16[128,4096]{1,0:T(8,128)(2,1)}) %all-gather.2.cloned.1.call-update) | async-done | bytes 1048592 | tf_op jit(solution)/shard_map/all_gather | solution.py:22
  53.7 8.3 %fusion.22 = bf16[128,2048]{1,0:T(8,128)(2,1)S(1)} fusion(bf16[128,4096]{1,0:T(8,128)(2,1)} %all-gather.2.cloned.1.call-done, bf16[1,4096,2048]{2,1,0:T(8,128)(2,1)} %param.14, f32[2048]{0:T(1024)} %bitcast.44), kind=kOutput, calls=%fused_computation.15 | convolution fusion | flops 2148270080 | bytes 18358272 | tf_op jit(solution)/shard_map/dot_general | solution.py:26
  62.1 0.0 copy-start.1
  62.1 13.0 %fusion = f32[128,8192]{1,0:T(8,128)S(1)} fusion(bf16[128,2048]{1,0:T(8,128)(2,1)S(1)} %fusion.22, bf16[1,2048,8192]{2,1,0:T(8,128)(2,1)} %param.16), kind=kOutput, calls=%fused_computation | convolution fusion | flops 4294967296 | bytes 38273024 | tf_op jit(solution)/shard_map/dot_general | solution.py:34
  75.1 0.0 copy-start
  75.1 1.9 copy-done
  77.0 0.0 copy-done.1
  77.1 8.2 %fusion.8 = f32[128,1792]{1,0:T(8,128)} fusion(bf16[128,4096]{1,0:T(8,128)(2,1)S(1)} %copy-done.1, bf16[1,4096,1792]{2,1,0:T(8,128)(2,1)} %param.11), kind=kOutput, calls=%fused_computation.8 | convolution fusion | flops 1879048192 | bytes 16646144 | tf_op jit(solution)/shard_map/dot_general | solution.py:23
  85.3 0.0 slice-start
  85.3 0.0 copy-start.2
  85.3 16.1 %fusion.10 = f32[128,4096]{1,0:T(8,128)} fusion(bf16[1,1792,4096]{2,1,0:T(8,128)(2,1)} %param.13, f32[128,8192]{1,0:T(8,128)} %copy-done, bf16[128,4096]{1,0:T(8,128)(2,1)S(1)} %copy-done.1, bf16[1,4096,1792]{2,1,0:T(8,128)(2,1)} %param.12, f32[128,1792]{1,0:T(8,128)} %fusion.8), kind=kOutput, calls=%fused_computation.10 | convolution fusion | flops 3759996928 | bytes 35520512 | tf_op jit(solution)/shard_map/dot_general | solution.py:35
  101.4 0.0 slice-done
  101.4 3.9 %pad_maximum_fusion = f32[128,8192]{1,0:T(8,128)} fusion(f32[128,4096]{1,0:T(8,128)S(1)} %slice-done, f32[128,4096]{1,0:T(8,128)} %fusion.10), kind=kLoop, calls=%fused_computation.11 | loop fusion | flops 1048576 | bytes 8388608 | tf_op jit(solution)/shard_map/concatenate | solution.py:37
  105.3 0.0 reduce-scatter.2.cloned.1.call-update
  105.3 87.2 %reduce-scatter.2.cloned.1.call-done = f32[16,8192]{1,0:T(8,128)} async-done(((f32[128,8192]{1,0:T(8,128)}), f32[16,8192]{1,0:T(8,128)}) %reduce-scatter.2.cloned.1.call-update) | async-done | bytes 524304 | tf_op jit(solution)/shard_map/reduce_scatter | solution.py:36
  192.4 1.7 slice_bitcast_fusion
  194.1 1.4 collective-permute-start
  195.5 1.1 collective-permute-done
  196.7 0.0 copy-done.2
  196.7 1.7 fusion.34
  (1 shorter events, 0.0 us)
Async XLA Ops:
  7.2 46.5 %all-gather.2.cloned.1.call-start = ((), (), s32[]{:S(2)}) async-start(), calls=%async_computation.1 | async-start | bytes 1179648 | tf_op jit(solution)/shard_map/all_gather | solution.py:22
  10.0 182.5 %reduce-scatter.2.cloned.1.call-start = ((), (), s32[]{:S(2)}) async-start(), calls=%async_computation.2 | async-start | bytes 4718592 | tf_op jit(solution)/shard_map/reduce_scatter | solution.py:36
  62.1 15.0 %copy-start.1 = (bf16[128,4096]{1,0:T(8,128)(2,1)S(1)}, bf16[128,4096]{1,0:T(8,128)(2,1)}, u32[]{:S(2)}) copy-start(bf16[128,4096]{1,0:T(8,128)(2,1)} %all-gather.2.cloned.1.call-done) | copy-start | bytes 3145732
  75.1 1.9 copy-start
  85.3 16.1 %slice-start = ((f32[128,8192]{1,0:T(8,128)}), f32[128,4096]{1,0:T(8,128)S(1)}, s32[]{:S(2)}) async-start(f32[128,8192]{1,0:T(8,128)} %copy-done), calls=%async_computation.3 | async-start | bytes 4194304 | tf_op jit(solution)/shard_map/slice | solution.py:37
  85.3 111.4 %copy-start.2 = (f32[16,4096]{1,0:T(8,128)S(1)}, f32[16,4096]{1,0:T(8,128)}, u32[]{:S(2)}) copy-start(f32[16,4096]{1,0:T(8,128)} %param.17) | copy-start | bytes 786436
  194.1 2.5 %collective-permute-start = (f32[16,4096]{1,0:T(8,128)S(1)}, f32[16,4096]{1,0:T(8,128)S(1)}, u32[]{:S(2)}, u32[]{:S(2)}) collective-permute-start(f32[16,4096]{1,0:T(8,128)S(1)} %get-tuple-element.3), channel_id=1, source_target_pairs={{0,8},{8,16},{16,24},{1,9},{9,17},{17,25},{2,10},{10,18},{18,26},{... | collective-permute-start | bytes 786440 | tf_op jit(solution)/shard_map/ppermute | solution.py:10
Sparse Core Ops, SparseCore 0:
  10.7 42.9 all-gather.1
  105.4 86.9 reduce-scatter.1
where the time goes:
time: 209 us; the launch traced here: 205 us
  waiting for transfers between devices  132 us (63%)
  matrix products  45.7 us (22%)
  between operations  14.1 us (7%)
  other arithmetic  8.3 us (4%)
  local copies, waits for them, and re-layouts  3.63 us (2%)
    reduce_scatter x1, waiting for transfers between devices, body(): lax.psum_scatter(jnp.concatenate([dec_part[:, :model_width] - mlp_part, d...  87.2 us
    all_gather x1, waiting for transfers between devices, body(): tile_rows = lax.all_gather(normed, 'feat', axis=0, tiled=True)  43.7 us
    dot_general x1, matrix products, body(): mlp_part = jnp.dot(hidden, down_rows, preferred_element_type=jnp.float32)  16.1 us
    dot_general x1, matrix products, body(): dec_part = jnp.dot(features, dec_rows, preferred_element_type=jnp.float32)  13 us
    dot_general x1, matrix products, body(): jnp.dot(tile_rows, enc_cols, preferred_element_type=jnp.float32) + enc_bias  8.34 us
    dot_general x1, matrix products, body(): gate_sum = jnp.dot(tile_rows, gate_cols, preferred_element_type=jnp.float32)  8.21 us
  transfers between devices with their start and end apart: 3, of which 3 were waited for; matrix products, arithmetic and copies ran while one was open for 0% of the time, Pallas kernels for 0%

commit v1 on v0

v1 whole, which is shorter than its diff:
```python
import functools

import jax
import jax.numpy as jnp
from jax import lax
from jax.experimental import pallas as pl
from jax.experimental.pallas import tpu as pltpu
from jax.sharding import PartitionSpec as P

MESH = pl.DeviceIdType.MESH
F32 = jnp.float32
BF16 = jnp.bfloat16


def chunk_of(width, want):
    size = want
    while size >= 128:
        if width % size == 0:
            return size
        size -= 128
    return width


def loop(count, body):
    if count == 1:
        body(0)
    else:
        lax.fori_loop(0, count, lambda i, c: (body(i), c)[1], 0)


def at(i, size):
    if isinstance(i, int):
        return pl.ds(i * size, size)
    return pl.ds(pl.multiple_of(i * size, size), size)


def kernel(cfg, resid, gain, w_gate, w_up, w_down, w_enc, b_enc, w_dec, carry, err_out, fwd_out,
           gbuf, ubuf, ebuf, dbuf, wbuf, xall, hidden, feats, keep, ysend, yrecv, zsend, zrecv, fsend, inc,
           gsem, usem, esem, dsem, wsem, agz_s, agz_r, agy_s, agy_r, ys_s, ys_r, zs_s, zs_r, fs_s, fs_r):
    G, Z, r, D, gw, ng, ew, ne, cw, nc = cfg
    nq = 2 * nc
    H = Z * r
    me = lax.axis_index("feat")
    g = lax.axis_index("grp")
    z = me // 2
    y = me - 2 * z
    partner = (g, 2 * z + 1 - y)
    sg, se, sd, sw = gbuf.shape[0], ebuf.shape[0], dbuf.shape[0], wbuf.shape[0]

    def peer(d):
        return (g, 2 * lax.rem(z + d, Z) + y)

    def gate_copy(c):
        s = c % sg
        return pltpu.make_async_copy(w_gate.at[0, :, at(c, gw)], gbuf.at[s], gsem.at[s])

    def up_copy(c):
        s = c % sg
        return pltpu.make_async_copy(w_up.at[0, :, at(c, gw)], ubuf.at[s], usem.at[s])

    def enc_copy(c):
        s = c % se
        return pltpu.make_async_copy(w_enc.at[0, :, at(c, ew)], ebuf.at[s], esem.at[s])

    def dec_copy(q):
        s = q % sd
        return pltpu.make_async_copy(w_dec.at[0, :, at((q + nc) % nq, cw)], dbuf.at[s], dsem.at[s])

    def down_copy(c):
        s = c % sw
        return pltpu.make_async_copy(w_down.at[0, :, at(c, cw)], wbuf.at[s], wsem.at[s])

    for c in range(sg):
        gate_copy(c).start()
        up_copy(c).start()
    for c in range(se):
        enc_copy(c).start()

    barrier = pltpu.get_barrier_semaphore()
    pl.semaphore_signal(barrier, inc=1, device_id=partner, device_id_type=MESH)
    for d in range(1, Z):
        pl.semaphore_signal(barrier, inc=1, device_id=peer(d), device_id_type=MESH)

    for near in (g + 1, g + G - 1):
        pl.semaphore_signal(barrier, inc=1, device_id=(lax.rem(near, G), me), device_id_type=MESH)

    stream = resid[0].astype(F32)
    inv_rms = lax.rsqrt(jnp.mean(stream * stream, axis=1, keepdims=True) + 1e-05)
    own = at(z, r)
    xall[own, :] = (stream * inv_rms * gain[...]).astype(BF16)

    pl.semaphore_wait(barrier, Z + 2)

    def rows_z(d):
        return at(lax.rem(z + Z - d, Z), r)

    def ag_z(d):
        return pltpu.make_async_remote_copy(
            src_ref=xall.at[own], dst_ref=xall.at[own], send_sem=agz_s.at[d - 1], recv_sem=agz_r.at[d - 1],
            device_id=peer(d), device_id_type=MESH)

    def ag_y(d):
        src = lax.rem(z + Z - d, Z)
        return pltpu.make_async_remote_copy(
            src_ref=xall.at[at(src, r)], dst_ref=xall.at[at(Z + src, r)], send_sem=agy_s.at[d], recv_sem=agy_r.at[d],
            device_id=partner, device_id_type=MESH)

    def ag_z_in(d):
        return pltpu.make_async_remote_copy(
            src_ref=xall.at[rows_z(d)], dst_ref=xall.at[rows_z(d)], send_sem=agz_s.at[d - 1], recv_sem=agz_r.at[d - 1],
            device_id=peer(d), device_id_type=MESH)

    for d in range(1, Z):
        ag_z(d).start()
    ag_y(0).start()
    for q in range(sd):
        dec_copy(q).start()
    for c in range(sw):
        down_copy(c).start()
    for d in range(1, Z):
        ag_z_in(d).wait_recv()
        ag_y(d).start()
    for d in range(Z):
        ag_y(d).wait_recv()

    def gate_up(c):
        gate_copy(c).wait()
        up_copy(c).wait()
        s = c % sg
        x = xall[...]
        gate = jnp.dot(x, gbuf[s], preferred_element_type=F32)
        up = jnp.dot(x, ubuf[s], preferred_element_type=F32)
        hidden[:, at(c, gw)] = (jax.nn.silu(gate) * up).astype(BF16)
        if ng > sg:
            @pl.when(c + sg < ng)
            def _():
                gate_copy(c + sg).start()
                up_copy(c + sg).start()

    def encode(c):
        enc_copy(c).wait()
        pre = jnp.dot(xall[...], ebuf[c % se], preferred_element_type=F32) + b_enc[:, at(c, ew)]
        feats[:, at(c, ew)] = jnp.maximum(pre, 0.0).astype(BF16)
        if ne > se:
            @pl.when(c + se < ne)
            def _():
                enc_copy(c + se).start()

    loop(ng, gate_up)
    loop(ne, encode)

    def y_copy(q):
        return pltpu.make_async_remote_copy(
            src_ref=ysend.at[q], dst_ref=yrecv.at[q], send_sem=ys_s.at[q], recv_sem=ys_r.at[q],
            device_id=partner, device_id_type=MESH)

    def z_copy(q, d):
        return pltpu.make_async_remote_copy(
            src_ref=zsend.at[q, at(lax.rem(z + d, Z), r)], dst_ref=zrecv.at[q, d - 1],
            send_sem=zs_s.at[q, d - 1], recv_sem=zs_r.at[q, d - 1], device_id=peer(d), device_id_type=MESH)

    def f_copy(c):
        return pltpu.make_async_remote_copy(
            src_ref=fsend.at[c], dst_ref=inc.at[c], send_sem=fs_s.at[c], recv_sem=fs_r.at[c],
            device_id=(lax.rem(g + 1, G), me), device_id_type=MESH)

    def split_out(q, part):
        keep[q] = part[:H]
        ysend[q] = part[H:].astype(BF16)
        y_copy(q).start()

    def produce(q):
        dec_copy(q).wait()
        part = jnp.dot(feats[...], dbuf[q % sd], preferred_element_type=F32)

        @pl.when(q < nc)
        def _():
            split_out(q, part)

        @pl.when(q >= nc)
        def _():
            c = q - nc
            down_copy(c).wait()
            split_out(q, part - jnp.dot(hidden[...], wbuf[c % sw], preferred_element_type=F32))

            @pl.when(c + sw < nc)
            def _():
                down_copy(c + sw).start()

        @pl.when(q + sd < nq)
        def _():
            dec_copy(q + sd).start()

    def pass_on(q):
        y_copy(q).wait_recv()
        both = keep[q] + yrecv[q].astype(F32)
        keep[q] = both
        zsend[q] = both.astype(BF16)
        for d in range(1, Z):
            z_copy(q, d).start()

    def finish(q):
        total = keep[q, own, :]
        for d in range(1, Z):
            z_copy(q, d).wait_recv()
            total = total + zrecv[q, d - 1].astype(F32)

        @pl.when(q < nc)
        def _():
            fwd_out[0, :, at(q, cw)] = total

            @pl.when(g < G - 1)
            def _():
                fsend[q] = total
                f_copy(q).start()

        @pl.when(q >= nc)
        def _():
            c = q - nc

            @pl.when(g == 0)
            def _():
                err_out[0, :, at(c, cw)] = total + carry[:, at(c, cw)]

            @pl.when(g > 0)
            def _():
                f_copy(c).wait_recv()
                err_out[0, :, at(c, cw)] = total + inc[c]

    lag_z, lag_f = 2, 4

    def step(t):
        @pl.when(t < nq)
        def _():
            produce(t)

        @pl.when((t >= lag_z) & (t < nq + lag_z))
        def _():
            pass_on(t - lag_z)

        @pl.when(t >= lag_f)
        def _():
            finish(t - lag_f)

    loop(nq + lag_f, step)

    for d in range(1, Z):
        ag_z(d).wait_send()
    for d in range(Z):
        ag_y(d).wait_send()

    def drain(q):
        y_copy(q).wait_send()
        for d in range(1, Z):
            z_copy(q, d).wait_send()

        @pl.when((q < nc) & (g < G - 1))
        def _():
            f_copy(q).wait_send()

    loop(nq, drain)


def solution(mesh):
    G, n = mesh.shape["grp"], mesh.shape["feat"]
    Z = n // 2

    def body(resid, norm_gain, w_gate, w_up, w_down, w_enc, b_enc, w_dec, carry_in):
        _, r, D = resid.shape
        fw, en = w_gate.shape[2], w_enc.shape[2]
        gw, ew = chunk_of(fw, 256), chunk_of(en, 256)
        ng, ne = fw // gw, en // ew
        cw = chunk_of(D, 512 if n <= 8 else 2048)
        nc = D // cw
        nq = 2 * nc
        H, T = Z * r, 2 * Z * r
        sg, se, sd, sw = min(4, ng), min(6, ne), min(6, nq), min(4, nc)
        cfg = (G, Z, r, D, gw, ng, ew, ne, cw, nc)
        vm = pl.BlockSpec(memory_space=pltpu.VMEM)
        hbm = pl.BlockSpec(memory_space=pl.ANY)
        sem = lambda *s: pltpu.SemaphoreType.DMA(s)
        return pl.pallas_call(
            functools.partial(kernel, cfg),
            out_shape=(jax.ShapeDtypeStruct((1, r, D), F32), jax.ShapeDtypeStruct((1, r, D), F32)),
            in_specs=[vm, vm, hbm, hbm, hbm, hbm, vm, hbm, vm],
            out_specs=(vm, vm),
            scratch_shapes=[
                pltpu.VMEM((sg, D, gw), BF16),
                pltpu.VMEM((sg, D, gw), BF16),
                pltpu.VMEM((se, D, ew), BF16),
                pltpu.VMEM((sd, en, cw), BF16),
                pltpu.VMEM((sw, fw, cw), BF16),
                pltpu.VMEM((T, D), BF16),
                pltpu.VMEM((T, fw), BF16),
                pltpu.VMEM((T, en), BF16),
                pltpu.VMEM((nq, H, cw), F32),
                pltpu.VMEM((nq, H, cw), BF16),
                pltpu.VMEM((nq, H, cw), BF16),
                pltpu.VMEM((nq, H, cw), BF16),
                pltpu.VMEM((nq, Z - 1, r, cw), BF16),
                pltpu.VMEM((nc, r, cw), F32),
                pltpu.VMEM((nc, r, cw), F32),
                sem(sg), sem(sg), sem(se), sem(sd), sem(sw),
                sem(Z - 1), sem(Z - 1), sem(Z), sem(Z),
                sem(nq), sem(nq), sem(nq, Z - 1), sem(nq, Z - 1), sem(nc), sem(nc),
            ],
            compiler_params=pltpu.CompilerParams(
                collective_id=0, has_side_effects=True, vmem_limit_bytes=67043328),
        )(resid, norm_gain, w_gate, w_up, w_down, w_enc, b_enc, w_dec, carry_in)

    return jax.shard_map(
        body,
        mesh=mesh,
        in_specs=(
            P("grp", "feat", None),
            P("grp", None),
            P("grp", None, "feat"),
            P("grp", None, "feat"),
            P("grp", "feat", None),
            P("grp", None, "feat"),
            P("grp", "feat"),
            P("grp", "feat", None),
            P("feat", None),
        ),
        out_specs=(P("grp", "feat", None), P("grp", "feat", None)),
        check_vma=False,
    )
```

time: 209 us -> 74.5 us (0.36); the launches traced: 205 us -> 74.3 us
  waiting for transfers between devices: 132 us -> 0 us
  Pallas kernels: 0 us -> 70.3 us
  matrix products: 45.7 us -> 0 us
  between operations: 14.1 us -> 0.64 us
  other arithmetic: 8.3 us -> 0 us
    reduce_scatter x1 -> x0, waiting for transfers between devices: 87.2 us -> none  [body(): lax.psum_scatter(jnp.concatenate([dec_part[:, :model_width] - mlp_part, d...]
    pallas_call x0 -> x1, Pallas kernels: none -> 70.3 us  [body(): pl.pallas_call(functools.partial(kernel, cfg), out_shape=(jax.ShapeDtypeS...]
    dot_general x4 -> x0, matrix products: 45.7 us -> none  [the longest x1 16.1 us: body(): mlp_part = jnp.dot(hidden, down_rows, preferred_element_type=jnp.float32)]
    all_gather x1 -> x0, waiting for transfers between devices: 43.7 us -> none  [body(): tile_rows = lax.all_gather(normed, 'feat', axis=0, tiled=True)]
    concatenate x1 -> x0, other arithmetic: 3.88 us -> none  [body(): jnp.concatenate([dec_part[:, :model_width] - mlp_part, dec_part[:, model_...]
  transfers between devices with their start and end apart: 3 -> 0, of which waited for: 3 -> 0; matrix products, arithmetic and copies ran while one was open for 0% -> 0% of each run, Pallas kernels for 0% -> 0%
where the time goes in v1:
time: 74.5 us; the launch traced here: 74.3 us
  Pallas kernels  70.3 us (94%)
  local copies, waits for them, and re-layouts  3.34 us (4%)
    pallas_call x1, Pallas kernels, body(): pl.pallas_call(functools.partial(kernel, cfg), out_shape=(jax.ShapeDtypeS...  70.3 us
    unnamed x2, local copies, waits for them, and re-layouts  3.34 us

profile of v1, /device:TPU:0, one launch (start us, length us, event | category | flops | bytes accessed | tf_op | source)
XLA Modules:
  0.0 74.3 jit_solution(14730530002514737394)
XLA Ops:
  0.6 70.3 %shard_map.104 = (f32[1,16,4096]{2,1,0:T(8,128)}, f32[1,16,4096]{2,1,0:T(8,128)}) custom-call(bf16[1,16,4096]{2,1,0:T(8,128)(2,1)} %resid.1, f32[1,4096]{1,0:T(1,128)} %gain.1, bf16[1,4096,1792]{2,1,0:T(8,128)(2,1)} %w_gate.1, bf16[1,4096,1792]{2,1,0:T(8,128)(2,1)} %w_up.1, bf16[1,1792,4096]{2,1,0:T(8,128)(2,1)} %w_down.1, bf16[1,4096,2048]{2,1,0:T(8,128)(2,1)} %w_enc.1, ...), custom_call_target="tpu_custom_call" | custom-call | tf_op jit(solution)/shard_map/pallas_call | solution.py:282
  70.9 1.7 %copy.13 = f32[1,16,4096]{2,1,0:T(8,128)} copy(f32[1,16,4096]{2,1,0:T(8,128)} %get-tuple-element.4) | data formatting | bytes 524288
  72.6 1.7 %copy.14 = f32[1,16,4096]{2,1,0:T(8,128)} copy(f32[1,16,4096]{2,1,0:T(8,128)} %get-tuple-element.5) | data formatting | bytes 524288
